TPU v7x, 16 devices: a 4x2x1 block of a 4x4x8 slice. The times are simulated.
16 devices in a mesh: dp: 2 (over y, z), tp: 8 (over x, core).
Axes of the slice: x: 4, y: 2, z: 1, core: 2. Of those that a mesh axis runs over, the one named last changes fastest.
The devices are a block of a 4x4x8 slice.
Arguments:
- x: bfloat16 [4096, 8192], P('dp'), parts along dimension 0
- w_gate: bfloat16 [8192, 32768], P(None, 'tp')
- w_up: bfloat16 [8192, 32768], P(None, 'tp')
- w_down: bfloat16 [32768, 8192], P('tp')
Outputs:
- output: bfloat16 [4096, 8192], P('dp'), parts along dimension 0
There are 2 independent parts. A program takes and returns all parts, laid end to end along the dimension named above; an argument that names none is the same for every part.
All inputs are finite; a program needn't handle non-finite values.
Results may differ from a plain program's by a relative error of at most 0.016.
Values are sent between devices in bfloat16 or wider.
A program may use at most 768 MiB of HBM per device.

v0:
```python
import jax
import jax.numpy as jnp
from jax import lax
from jax.sharding import PartitionSpec as P


def solution(mesh):
    def step(x, w_gate, w_up, w_down):
        gate = jnp.dot(x, w_gate, preferred_element_type=jnp.float32)
        up = jnp.dot(x, w_up, preferred_element_type=jnp.float32)
        hidden = (jax.nn.silu(gate) * up).astype(jnp.bfloat16)
        term = jnp.dot(hidden, w_down, preferred_element_type=jnp.float32).astype(jnp.bfloat16)
        return lax.psum(term, "tp")

    return jax.shard_map(
        step,
        mesh=mesh,
        in_specs=(P("dp", None), P(None, "tp"), P(None, "tp"), P("tp", None)),
        out_specs=P("dp", None),
        check_vma=False,
    )
```

profile of v0, /device:TPU:113, one launch (start us, length us, event | category | flops | bytes accessed | tf_op | source)
XLA Modules:
  0.0 834.6 jit_solution(16663973858831727046)
XLA Ops:
  6.5 0.0 all-reduce.2.cloned.1.call-start
  6.6 152.0 %fusion = f32[2048,4096]{1,0:T(8,128)} fusion(bf16[2048,8192]{1,0:T(8,128)(2,1)} %param.4, bf16[8192,4096]{1,0:T(8,128)(2,1)} %param.5), kind=kOutput, calls=%fused_computation.2 | convolution fusion | flops 137438953472 | bytes 134217728 | tf_op jit(solution)/shard_map/dot_general | solution.py:9
  158.6 160.3 %multiply_convert_fusion = bf16[2048,4096]{1,0:T(8,128)(2,1)} fusion(f32[2048,4096]{1,0:T(8,128)} %fusion, bf16[2048,8192]{1,0:T(8,128)(2,1)} %param.4, bf16[8192,4096]{1,0:T(8,128)(2,1)} %param.6), kind=kOutput, calls=%fused_computation | convolution fusion | flops 137489285120 | bytes 150994944 | tf_op jit(solution)/shard_map/dot_general | solution.py:10
  318.8 151.2 %convolution_convert_fusion = bf16[2048,8192]{1,0:T(8,128)(2,1)} fusion(bf16[2048,4096]{1,0:T(8,128)(2,1)} %multiply_convert_fusion, bf16[4096,8192]{1,0:T(8,128)(2,1)} %param.7), kind=kOutput, calls=%fused_computation.1 | convolution fusion | flops 137455730688 | bytes 117440512 | tf_op jit(solution)/shard_map/dot_general | solution.py:12
  470.0 0.1 all-reduce.2.cloned.1.call-update
  470.1 334.7 %all-reduce.2.cloned.1.call-done = bf16[2048,8192]{1,0:T(8,128)(2,1)} async-done(((bf16[2048,8192]{1,0:T(8,128)(2,1)}), bf16[2048,8192]{1,0:T(8,128)(2,1)}) %all-reduce.2.cloned.1.call-update) | async-done | bytes 33554448 | tf_op jit(solution)/shard_map/psum | solution.py:13
  804.8 23.0 %copy.6 = bf16[2048,8192]{1,0:T(8,128)(2,1)} copy(bf16[2048,8192]{1,0:T(8,128)(2,1)} %all-reduce.2.cloned.1.call-done) | data formatting | bytes 67108864
Async XLA Ops:
  6.5 798.3 %all-reduce.2.cloned.1.call-start = ((), (), s32[]{:S(2)}) async-start(), calls=%async_computation | async-start | bytes 67108864 | tf_op jit(solution)/shard_map/psum | solution.py:13
Sparse Core Ops, SparseCore 0:
  470.2 334.5 all-reduce.1
where the time goes:
time: 835 us
  matrix products  463 us (55%)
  waiting for transfers between devices  335 us (40%)
  local copies, waits for them, and re-layouts  23 us (3%)
  between operations  13.4 us (2%)
    psum x1, waiting for transfers between devices, step(): return lax.psum(term, 'tp')  335 us
    dot_general x1, matrix products, step(): up = jnp.dot(x, w_up, preferred_element_type=jnp.float32)  160 us
    dot_general x1, matrix products, step(): gate = jnp.dot(x, w_gate, preferred_element_type=jnp.float32)  152 us
    dot_general x1, matrix products, step(): jnp.dot(hidden, w_down, preferred_element_type=jnp.float32)  151 us
    unnamed x1, local copies, waits for them, and re-layouts  23 us
  transfers between devices with their start and end apart: 1, of which 1 were waited for; matrix products, arithmetic and copies ran while one was open for 0% of the time, Pallas kernels for 0%

commit v1 on v0

v1 whole, which is shorter than its diff:
```python
import functools

import jax
import jax.numpy as jnp
from jax import lax
from jax.experimental import pallas as pl
from jax.experimental.pallas import tpu as pltpu
from jax.sharding import PartitionSpec as P

MESH = pl.DeviceIdType.MESH
BF16, F32 = jnp.bfloat16, jnp.float32

CHUNK = 512
GU = 256
DN = 512

OTHER, OWN = 0, 1
ORDER = (
    (OTHER, 2, 0), (OTHER, 2, 1), (OTHER, 3, 0), (OWN, 2, 0), (OWN, 2, 1), (OTHER, 3, 1), (OTHER, 1, 0), (OTHER, 1, 1),
    (OWN, 3, 1), (OWN, 1, 0), (OTHER, 0, 0), (OTHER, 0, 1), (OWN, 3, 0), (OWN, 1, 1), (OWN, 0, 0), (OWN, 0, 1),
)
TILES = len(ORDER)
STAGED = TILES - 2
RING = {3: (-1, 0), 4: (1, 1), 8: (-1, 3), 9: (1, 4), 12: (-1, 2), 13: (1, 5)}
FIRST = 2


def pick(t, values):
    out = jnp.int32(values[0])
    for k, v in enumerate(values[1:], 1):
        if v != values[0]:
            out = jnp.where(t == k, jnp.int32(v), out)
    return out


def kernel(chips, chunks, x_ref, wg_ref, wu_ref, wd_ref, y_ref, x_v, hid, wg_v, wu_v, wd_v, g0, u0, g1, u1, a0, a1,
           other, hop1, hop2, stage, fin, x_sem, wg_sem, wu_sem, wd_sem, send_sem, other_sem, ring_sem, gsend_sem,
           gather_sem, credit):
    dp, tp = lax.axis_index("dp"), lax.axis_index("tp")
    chip, core = tp // 2, tp % 2
    nxt, prv = (chip + 1) % chips, (chip + chips - 1) % chips
    far = (chip + 2) % chips
    dev_next, dev_prev, dev_other = (dp, nxt * 2 + core), (dp, prv * 2 + core), (dp, chip * 2 + 1 - core)
    n_gu = wg_ref.shape[1] // GU
    last = chunks - 1

    barrier = pltpu.get_barrier_semaphore()
    for dev in (dev_next, dev_prev, dev_other):
        pl.semaphore_signal(barrier, inc=1, device_id=dev, device_id_type=MESH)
    pl.semaphore_wait(barrier, 3)

    def rows(chunk):
        return pl.ds(pl.multiple_of(chunk * CHUNK, CHUNK), CHUNK)

    def x_copy(chunk):
        return pltpu.make_async_copy(x_ref.at[rows(chunk), :], x_v, x_sem)

    def gu_copies(j, slot):
        cols = pl.ds(pl.multiple_of(j * GU, GU), GU)
        return (pltpu.make_async_copy(wg_ref.at[:, cols], wg_v.at[slot], wg_sem.at[slot]),
                pltpu.make_async_copy(wu_ref.at[:, cols], wu_v.at[slot], wu_sem.at[slot]))

    def block(half, owner, piece):
        return (half * chips + owner) * 2 + piece

    def wd_copy(t, slot):
        half = jnp.where(pick(t, [o[0] for o in ORDER]) == OWN, core, 1 - core)
        owner = (chip + pick(t, [o[1] for o in ORDER])) % chips
        tile = block(half, owner, pick(t, [o[2] for o in ORDER]))
        cols = pl.ds(pl.multiple_of(tile * DN, DN), DN)
        return pltpu.make_async_copy(wd_ref.at[:, cols], wd_v.at[slot], wd_sem.at[slot])

    def remote(src, dst, send, recv, dev):
        return pltpu.make_async_remote_copy(src_ref=src, dst_ref=dst, send_sem=send, recv_sem=recv, device_id=dev,
                                            device_id_type=MESH)

    def other_copy(chunk, t, slot):
        return remote(stage.at[t], other.at[slot], send_sem.at[t], other_sem.at[chunk, slot], dev_other)

    def ring_copy(chunk, t):
        direction, slot = RING[t]
        dst = hop1.at[slot] if slot < FIRST else hop2.at[slot - FIRST]
        return remote(stage.at[t], dst, send_sem.at[t], ring_sem.at[chunk, slot], dev_next if direction > 0 else dev_prev)

    def out(chunk, owner, half=core, piece=None):
        if piece is None:
            return y_ref.at[rows(chunk), pl.ds(pl.multiple_of(block(half, owner, 0) * DN, 2 * DN), 2 * DN)]
        return y_ref.at[rows(chunk), pl.ds(pl.multiple_of(block(half, owner, piece) * DN, DN), DN)]

    def gathers(chunk):
        def put(src, dst, k, slot, dev):
            return remote(src, dst, gsend_sem.at[k], gather_sem.at[chunk, slot], dev)

        mine = out(chunk, chip)
        first = (put(fin, mine, 1, 4, dev_other), put(fin, mine, 2, 0, dev_next), put(fin, mine, 3, 1, dev_prev))
        a, b = out(chunk, prv, piece=0), out(chunk, nxt, piece=1)
        p, n = out(chunk, prv), out(chunk, nxt)
        second = (put(a, a, 4, 2, dev_next), put(b, b, 5, 3, dev_prev), put(p, p, 6, 5, dev_other),
                  put(n, n, 7, 6, dev_other))
        fa, fb = out(chunk, far, piece=0), out(chunk, far, piece=1)
        third = (put(fa, fa, 8, 7, dev_other), put(fb, fb, 9, 8, dev_other))
        return pltpu.make_async_copy(fin, mine, gsend_sem.at[0]), first, second, third

    def gather_wait(chunk, slot, dst):
        remote(dst, dst, gsend_sem.at[0], gather_sem.at[chunk, slot], dev_other).wait_recv()

    def sent(chunk):
        local, first, second, third = gathers(chunk)
        local.wait()
        for copy in first + second + third:
            copy.wait_send()

    def finish(chunk):
        for slot in range(2):
            remote(stage.at[0], other.at[slot], send_sem.at[0], other_sem.at[chunk, slot], dev_other).wait_recv()
        for k in range(4):
            remote(stage.at[0], hop2.at[k], send_sem.at[0], ring_sem.at[chunk, FIRST + k], dev_next).wait_recv()

        @pl.when(chunk > 0)
        def _():
            sent(chunk - 1)

        step = 64

        def strip(i, _):
            r = pl.ds(pl.multiple_of(i * step, step), step)
            for piece, acc in ((0, a0), (1, a1)):
                total = acc[r, :] + other[piece, r, :].astype(F32)
                total += hop2[piece, r, :].astype(F32)
                total += hop2[2 + piece, r, :].astype(F32)
                fin[r, piece * DN:(piece + 1) * DN] = total.astype(BF16)
            return 0

        lax.fori_loop(0, CHUNK // step, strip, 0)
        local, first, _, _ = gathers(chunk)
        for copy in (first[1], first[2], first[0], local):
            copy.start()

        @pl.when(chunk < last)
        def _():
            for k, dev in enumerate((dev_prev, dev_next, dev_other)):
                pl.semaphore_signal(credit.at[k], inc=1, device_id=dev, device_id_type=MESH)

    def forward1(chunk):
        gather_wait(chunk, 0, out(chunk, prv))
        gather_wait(chunk, 1, out(chunk, nxt))
        for copy in gathers(chunk)[2]:
            copy.start()

    def forward2(chunk):
        gather_wait(chunk, 2, out(chunk, far, piece=0))
        gather_wait(chunk, 3, out(chunk, far, piece=1))
        for copy in gathers(chunk)[3]:
            copy.start()

    def activate(g, u, j):
        cols = pl.ds(pl.multiple_of(j * GU, GU), GU)
        gate = g[...]
        hid[:, cols] = (gate * jax.nn.sigmoid(gate) * u[...]).astype(BF16)

    def gu_tile(slot, g, u, g_old, u_old, j_old):
        g[...] = jnp.dot(x_v[...], wg_v[slot], preferred_element_type=F32)
        u[...] = jnp.dot(x_v[...], wu_v[slot], preferred_element_type=F32)
        activate(g_old, u_old, j_old)

    def dn_tile(chunk, t, slot, acc, acc_old):
        old = t - 1
        staged = (old >= 0) & (old < STAGED)
        is_own = [o[0] == OWN for o in ORDER[:STAGED]]
        own = staged & (pick(old, [int(f) for f in is_own]) == 1)
        slots = [o[1] * 2 + o[2] for o in ORDER]
        arrived = pick(old, slots)

        @pl.when(staged & (chunk > 0))
        def _():
            remote(stage.at[old], other.at[0], send_sem.at[old], other_sem.at[chunk, 0], dev_other).wait_send()

        @pl.when(own)
        def _():
            remote(stage.at[0], other.at[arrived], send_sem.at[0], other_sem.at[chunk, arrived], dev_other).wait_recv()

        for k, at in ((0, 12), (1, 13)):
            @pl.when(old == at)
            def _(k=k):
                remote(stage.at[0], hop1.at[k], send_sem.at[0], ring_sem.at[chunk, k], dev_next).wait_recv()

        from_other = jnp.where(own, arrived, len(ORDER) // 2)
        from_ring = jnp.where(old == 12, 0, jnp.where(old == 13, 1, 2))
        to = jnp.where(staged, old, STAGED)
        acc[...] = jnp.dot(hid[...], wd_v[slot], preferred_element_type=F32)
        total = acc_old[...] + other[from_other].astype(F32) + hop1[from_ring].astype(F32)
        stage[to] = total.astype(BF16)

        @pl.when(staged & jnp.logical_not(own))
        def _():
            other_copy(chunk, old, arrived).start()

        for at in RING:
            @pl.when(old == at)
            def _(at=at):
                ring_copy(chunk, at).start()

    x_copy(0).start()
    for copy in gu_copies(0, 0):
        copy.start()
    other[len(ORDER) // 2] = jnp.zeros(other.shape[1:], BF16)
    hop1[FIRST] = jnp.zeros(hop1.shape[1:], BF16)

    def one_chunk(chunk, _):
        x_copy(chunk).wait()

        def gu_pair(i, _):
            j = i * 2
            for copy in gu_copies(j, 0):
                copy.wait()
            for copy in gu_copies(j + 1, 1):
                copy.start()
            gu_tile(0, g0, u0, g1, u1, (j + n_gu - 1) % n_gu)
            for copy in gu_copies(j + 1, 1):
                copy.wait()

            @pl.when(j + 2 < n_gu)
            def _():
                for copy in gu_copies(j + 2, 0):
                    copy.start()

            @pl.when(j + 2 >= n_gu)
            def _():
                wd_copy(jnp.int32(0), 0).start()

            for at, act in ((1, finish), (4, forward1), (6, forward2)):
                @pl.when((i == at) & (chunk > 0))
                def _(act=act):
                    act(chunk - 1)

            gu_tile(1, g1, u1, g0, u0, j)
            return 0

        lax.fori_loop(0, n_gu // 2, gu_pair, 0)
        activate(g1, u1, n_gu - 1)

        @pl.when(chunk > 0)
        def _():
            for k in range(3):
                pl.semaphore_wait(credit.at[k], 1)

        @pl.when(chunk < last)
        def _():
            x_copy(chunk + 1).start()

        def dn_pair(i, _):
            t = i * 2
            wd_copy(t, 0).wait()
            wd_copy(t + 1, 1).start()
            dn_tile(chunk, t, 0, a0, a1)
            wd_copy(t + 1, 1).wait()

            @pl.when(t + 2 < TILES)
            def _():
                wd_copy(t + 2, 0).start()

            @pl.when((t + 2 >= TILES) & (chunk < last))
            def _():
                for copy in gu_copies(0, 0):
                    copy.start()

            dn_tile(chunk, t + 1, 1, a1, a0)
            return 0

        lax.fori_loop(0, TILES // 2, dn_pair, 0)
        return 0

    lax.fori_loop(0, chunks, one_chunk, 0)
    finish(last)
    forward1(last)
    forward2(last)
    sent(last)
    for t in range(STAGED):
        remote(stage.at[t], other.at[0], send_sem.at[t], other_sem.at[last, 0], dev_other).wait_send()
    for chunk in range(chunks):
        half = 1 - core
        for slot, dst in ((4, out(chunk, chip, half)), (5, out(chunk, prv, half)), (6, out(chunk, nxt, half)),
                          (7, out(chunk, far, half, 0)), (8, out(chunk, far, half, 1))):
            gather_wait(chunk, slot, dst)


def solution(mesh):
    chips = mesh.shape["tp"] // 2

    def step(x, w_gate, w_up, w_down):
        n, d = x.shape
        ff = w_gate.shape[1]
        chunks = n // CHUNK
        dma = pltpu.SemaphoreType.DMA
        hbm = pl.BlockSpec(memory_space=pl.ANY)
        return pl.pallas_call(
            functools.partial(kernel, chips, chunks),
            out_shape=jax.ShapeDtypeStruct((n, d), BF16),
            in_specs=[hbm] * 4,
            out_specs=hbm,
            scratch_shapes=[
                pltpu.VMEM((CHUNK, d), BF16),
                pltpu.VMEM((CHUNK, ff), BF16),
                pltpu.VMEM((2, d, GU), BF16),
                pltpu.VMEM((2, d, GU), BF16),
                pltpu.VMEM((2, ff, DN), BF16),
                *[pltpu.VMEM((CHUNK, GU), F32)] * 4,
                *[pltpu.VMEM((CHUNK, DN), F32)] * 2,
                pltpu.VMEM((TILES // 2 + 1, CHUNK, DN), BF16),
                pltpu.VMEM((FIRST + 1, CHUNK, DN), BF16),
                pltpu.VMEM((4, CHUNK, DN), BF16),
                pltpu.VMEM((STAGED + 1, CHUNK, DN), BF16),
                pltpu.VMEM((CHUNK, 2 * DN), BF16),
                dma, dma((2,)), dma((2,)), dma((2,)),
                dma((STAGED,)),
                dma((chunks, TILES // 2)),
                dma((chunks, FIRST + 4)),
                dma((10,)),
                dma((chunks, 9)),
                pltpu.SemaphoreType.REGULAR((3,)),
            ],
            compiler_params=pltpu.CompilerParams(
                collective_id=0, has_side_effects=True, vmem_limit_bytes=67043328),
            cost_estimate=pl.CostEstimate(flops=6 * n * d * ff, bytes_accessed=chunks * 6 * d * ff, transcendentals=n * ff),
        )(x, w_gate, w_up, w_down)

    return jax.shard_map(
        step,
        mesh=mesh,
        in_specs=(P("dp", None), P(None, "tp"), P(None, "tp"), P("tp", None)),
        out_specs=P("dp", None),
        check_vma=False,
    )
```

time: 835 us -> 562 us (0.67)
  Pallas kernels: 0 us -> 539 us
  matrix products: 463 us -> 0 us
  waiting for transfers between devices: 335 us -> 0 us
  between operations: 13.4 us -> 0.01 us
    pallas_call x0 -> x1, Pallas kernels: none -> 539 us  [step(): pl.pallas_call(functools.partial(kernel, chips, chunks), out_shape=jax.Sh...]
    dot_general x3 -> x0, matrix products: 463 us -> none  [the longest x1 160 us: step(): up = jnp.dot(x, w_up, preferred_element_type=jnp.float32)]
    psum x1 -> x0, waiting for transfers between devices: 335 us -> none  [step(): return lax.psum(term, 'tp')]
  transfers between devices with their start and end apart: 1 -> 0, of which waited for: 1 -> 0; matrix products, arithmetic and copies ran while one was open for 0% -> 0% of each run, Pallas kernels for 0% -> 0%
where the time goes in v1:
time: 562 us
  Pallas kernels  539 us (96%)
  local copies, waits for them, and re-layouts  23 us (4%)
    pallas_call x1, Pallas kernels, step(): pl.pallas_call(functools.partial(kernel, chips, chunks), out_shape=jax.Sh...  539 us
    unnamed x1, local copies, waits for them, and re-layouts  23 us

profile of v1, /device:TPU:113, one launch (start us, length us, event | category | flops | bytes accessed | tf_op | source)
XLA Modules:
  0.0 561.9 jit_solution(4807134656997487100)
XLA Ops:
  0.0 538.9 %shard_map.46 = bf16[2048,8192]{1,0:T(8,128)(2,1)} custom-call(bf16[2048,8192]{1,0:T(8,128)(2,1)} %x_ref.1, bf16[8192,4096]{1,0:T(8,128)(2,1)} %wg_ref.1, bf16[8192,4096]{1,0:T(8,128)(2,1)} %wu_ref.1, bf16[4096,8192]{1,0:T(8,128)(2,1)} %wd_ref.1), custom_call_target="tpu_custom_call" | custom-call | flops 412316860416 | bytes 805306368 | tf_op jit(solution)/shard_map/pallas_call | solution.py:296
  538.9 23.0 %copy.6 = bf16[2048,8192]{1,0:T(8,128)(2,1)} copy(bf16[2048,8192]{1,0:T(8,128)(2,1)} %shard_map.46) | data formatting | bytes 67108864

commit v2 on v0

v2 whole, which is shorter than its diff:
```python
import functools

import jax
import jax.numpy as jnp
from jax import lax
from jax.experimental import pallas as pl
from jax.experimental.pallas import tpu as pltpu
from jax.sharding import PartitionSpec as P

MESH = pl.DeviceIdType.MESH
BF16, F32 = jnp.bfloat16, jnp.float32

GU = 256
DN = 512
SHARES = (18, 18, 17, 11)
SLOTS = 6

OTHER, OWN = 0, 1
ORDER = (
    (OTHER, 2, 0), (OTHER, 2, 1), (OTHER, 3, 0), (OWN, 2, 0), (OWN, 2, 1), (OTHER, 3, 1), (OTHER, 1, 0), (OTHER, 1, 1),
    (OWN, 3, 1), (OWN, 1, 0), (OTHER, 0, 0), (OTHER, 0, 1), (OWN, 3, 0), (OWN, 1, 1), (OWN, 0, 0), (OWN, 0, 1),
)
TILES = len(ORDER)
STAGED = TILES - 2
STAGE = (0, 1, 0, 2, 3, 1, 0, 1, 4, 5, 0, 1, 6, 7)
REUSED = tuple(int(slot in STAGE[:t]) for t, slot in enumerate(STAGE))
STAGES = max(STAGE) + 1
RING = {3: (-1, 0), 4: (1, 1), 8: (-1, 3), 9: (1, 4), 12: (-1, 2), 13: (1, 5)}
FIRST = 2


def pick(t, values):
    out = jnp.int32(values[0])
    for k, v in enumerate(values[1:], 1):
        if v != values[0]:
            out = jnp.where(t == k, jnp.int32(v), out)
    return out


def kernel(chips, sizes, x_ref, wg_ref, wu_ref, wd_ref, y_ref, x_v, hid, w_v, kept, other, hop1, hop2, stage, fin,
           x_sem, w_sem, send_sem, other_sem, ring_sem, gsend_sem, gather_sem, credit):
    dp, tp = lax.axis_index("dp"), lax.axis_index("tp")
    chip, core = tp // 2, tp % 2
    nxt, prv = (chip + 1) % chips, (chip + chips - 1) % chips
    far = (chip + 2) % chips
    dev_next, dev_prev, dev_other = (dp, nxt * 2 + core), (dp, prv * 2 + core), (dp, chip * 2 + 1 - core)
    n_gu = wg_ref.shape[1] // GU
    ff = wd_ref.shape[0]
    chunks = len(sizes)
    starts = [sum(sizes[:k]) for k in range(chunks)]
    last = chunks - 1

    barrier = pltpu.get_barrier_semaphore()
    for dev in (dev_next, dev_prev, dev_other):
        pl.semaphore_signal(barrier, inc=1, device_id=dev, device_id_type=MESH)
    pl.semaphore_wait(barrier, 3)

    def x_copy(c):
        return pltpu.make_async_copy(x_ref.at[pl.ds(starts[c], sizes[c]), :], x_v.at[pl.ds(0, sizes[c]), :], x_sem)

    def w_copy(src, j, slot):
        cols = pl.ds(pl.multiple_of(j * GU, GU), GU)
        return pltpu.make_async_copy(src.at[:, cols], w_v.at[slot], w_sem.at[slot])

    def block(half, owner, piece):
        return (half * chips + owner) * 2 + piece

    def wd_load(t):
        slot = (2 * n_gu + t) % SLOTS
        half = jnp.where(pick(t, [o[0] for o in ORDER]) == OWN, core, 1 - core)
        owner = (chip + pick(t, [o[1] for o in ORDER])) % chips
        tile = block(half, owner, pick(t, [o[2] for o in ORDER]))
        for k in range(2):
            cols = pl.ds(pl.multiple_of(tile * DN + k * GU, GU), GU)
            pltpu.make_async_copy(wd_ref.at[:, cols], w_v.at[slot, pl.ds(k * ff, ff), :], w_sem.at[slot]).start()

    def w_wait(slot):
        w_copy(wg_ref, 0, slot).wait()

    def gu_load(j):
        for k, src in enumerate((wg_ref, wu_ref)):
            w_copy(src, j, (2 * j + k) % SLOTS).start()

    def remote(src, dst, send, recv, dev):
        return pltpu.make_async_remote_copy(src_ref=src, dst_ref=dst, send_sem=send, recv_sem=recv, device_id=dev,
                                            device_id_type=MESH)

    def top(ref, k, c):
        return ref.at[k, pl.ds(0, sizes[c]), :]

    def other_copy(c, t, slot):
        at = pick(t, STAGE)
        return remote(top(stage, at, c), top(other, slot, c), send_sem.at[at], other_sem.at[c, slot], dev_other)

    def ring_copy(c, t):
        direction, slot = RING[t]
        dst = top(hop1, slot, c) if slot < FIRST else top(hop2, slot - FIRST, c)
        return remote(top(stage, STAGE[t], c), dst, send_sem.at[STAGE[t]], ring_sem.at[c, slot],
                      dev_next if direction > 0 else dev_prev)

    def stage_sent(c, slot):
        remote(top(stage, slot, c), top(other, 0, c), send_sem.at[slot], other_sem.at[c, 0], dev_other).wait_send()

    def out(c, owner, half=None, piece=None):
        half = core if half is None else half
        r = pl.ds(starts[c], sizes[c])
        if piece is None:
            return y_ref.at[r, pl.ds(pl.multiple_of(block(half, owner, 0) * DN, 2 * DN), 2 * DN)]
        return y_ref.at[r, pl.ds(pl.multiple_of(block(half, owner, piece) * DN, DN), DN)]

    def gather(c, k):
        def put(src, dst, dev):
            return remote(src, dst, gsend_sem.at[k], gather_sem.at[c, k], dev)

        def mine(piece):
            return fin.at[pl.ds(0, sizes[c]), pl.ds(piece * DN, DN)], out(c, chip, piece=piece)

        if k < 4:
            piece, dev = ((0, dev_next), (1, dev_prev), (1, dev_next), (0, dev_prev))[k]
            return put(*mine(piece), dev)
        if k == 4:
            return put(fin.at[pl.ds(0, sizes[c]), :], out(c, chip), dev_other)
        if k < 7:
            owner, piece, dev = ((prv, 0, dev_next), (nxt, 1, dev_prev))[k - 5]
        else:
            owner, piece, dev = ((prv, None, dev_other), (nxt, None, dev_other), (far, 0, dev_other),
                                 (far, 1, dev_other))[k - 7]
        ref = out(c, owner, piece=piece)
        return put(ref, ref, dev)

    def gather_wait(c, k, dst):
        remote(dst, dst, gsend_sem.at[k], gather_sem.at[c, k], dev_other).wait_recv()

    def local_copy(c):
        return pltpu.make_async_copy(fin.at[pl.ds(0, sizes[c]), :], out(c, chip), gsend_sem.at[11])

    def sent(c):
        local_copy(c).wait()
        for k in range(11):
            gather(c, k).wait_send()

    def finish(c):
        for slot in range(2):
            other_wait(c, slot)
        for k in range(4):
            ring_wait(c, FIRST + k)
        size, step = sizes[c], 32

        def strip(i, _):
            r = pl.ds(pl.multiple_of(i * step, step), step)
            for piece in range(2):
                total = kept[piece, r, :] + other[piece, r, :].astype(F32)
                total += hop2[piece, r, :].astype(F32)
                total += hop2[2 + piece, r, :].astype(F32)
                fin[r, piece * DN:(piece + 1) * DN] = total.astype(BF16)
            return 0

        lax.fori_loop(0, size // step, strip, 0)
        for k in range(5):
            gather(c, k).start()
        local_copy(c).start()
        for slot in range(STAGES):
            stage_sent(c, slot)
        if c < last:
            for k, dev in enumerate((dev_prev, dev_next, dev_other)):
                pl.semaphore_signal(credit.at[k], inc=1, device_id=dev, device_id_type=MESH)

    def other_wait(c, slot):
        remote(top(stage, 0, c), top(other, slot, c), send_sem.at[0], other_sem.at[c, slot], dev_other).wait_recv()

    def ring_wait(c, slot):
        dst = top(hop1, slot, c) if slot < FIRST else top(hop2, slot - FIRST, c)
        remote(top(stage, 0, c), dst, send_sem.at[0], ring_sem.at[c, slot], dev_next).wait_recv()

    def forward1(c):
        gather_wait(c, 0, out(c, prv, piece=0))
        gather(c, 5).start()
        gather_wait(c, 1, out(c, nxt, piece=1))
        gather(c, 6).start()
        gather_wait(c, 2, out(c, prv, piece=1))
        gather(c, 7).start()
        gather_wait(c, 3, out(c, nxt, piece=0))
        gather(c, 8).start()

    def forward2(c):
        gather_wait(c, 5, out(c, far, piece=0))
        gather(c, 9).start()
        gather_wait(c, 6, out(c, far, piece=1))
        gather(c, 10).start()

    x_copy(0).start()
    for j in range(SLOTS // 2):
        gu_load(j)
    other[TILES // 2] = jnp.zeros(other.shape[1:], BF16)
    hop1[FIRST] = jnp.zeros(hop1.shape[1:], BF16)

    def one_chunk(c):
        size = sizes[c]
        span = (3, 9, 13) if size * 4 >= sizes[c - 1] * 3 else (4, 13, 15)
        x_copy(c).wait()

        def gu_step(j, _):
            @pl.when(j > 0)
            def _():
                @pl.when(j + 2 < n_gu)
                def _():
                    gu_load(j + 2)

                @pl.when(j + 2 >= n_gu)
                def _():
                    wd_load(2 * (j + 2 - n_gu))
                    wd_load(2 * (j + 2 - n_gu) + 1)

            if c:
                @pl.when(j == 0)
                def _():
                    w_copy(wu_ref, 2, 5).start()

                for at, act in zip(span, (finish, forward1, forward2)):
                    @pl.when(j == at)
                    def _(act=act):
                        act(c - 1)

            a, b = (2 * j) % SLOTS, (2 * j + 1) % SLOTS
            w_wait(a)
            w_wait(b)
            rows = x_v[:size, :]
            gate = jnp.dot(rows, w_v[a], preferred_element_type=F32)
            up = jnp.dot(rows, w_v[b], preferred_element_type=F32)
            hid[:size, pl.ds(pl.multiple_of(j * GU, GU), GU)] = (gate * jax.nn.sigmoid(gate) * up).astype(BF16)
            return 0

        lax.fori_loop(0, n_gu, gu_step, 0)

        if c:
            sent(c - 1)
            for k in range(3):
                pl.semaphore_wait(credit.at[k], 1)
        if c < last:
            x_copy(c + 1).start()

        def dn_dots(t):
            slot = (2 * n_gu + t) % SLOTS

            @pl.when(t == 0)
            def _():
                wd_load(t + 4)
                wd_load(t + 5)

            @pl.when((t > 0) & (t + 5 < TILES))
            def _():
                wd_load(t + 5)

            if c < last:
                for m in range(SLOTS - 1):
                    @pl.when(t + 5 == TILES + m)
                    def _(m=m):
                        w_copy((wg_ref, wu_ref)[m % 2], m // 2, m).start()

            w_wait(slot)
            return [jnp.dot(hid[:size, :], w_v[slot, k * ff:(k + 1) * ff, :], preferred_element_type=F32)
                    for k in range(2)]

        def dn_step(t, _):
            own = pick(t, [o[0] for o in ORDER[:STAGED]]) == OWN
            arrived = pick(t, [o[1] * 2 + o[2] for o in ORDER[:STAGED]])
            to = pick(t, STAGE)

            @pl.when(pick(t, REUSED) == 1)
            def _():
                stage_sent(c, to)

            @pl.when(own)
            def _():
                other_wait(c, arrived)

            for k, at in ((0, 12), (1, 13)):
                @pl.when(t == at)
                def _(k=k):
                    ring_wait(c, k)

            from_other = jnp.where(own, arrived, TILES // 2)
            from_ring = jnp.where(t == 12, 0, jnp.where(t == 13, 1, FIRST))
            for k, part in enumerate(dn_dots(t)):
                cols = slice(k * GU, (k + 1) * GU)
                total = part + other[from_other, :size, cols].astype(F32) + hop1[from_ring, :size, cols].astype(F32)
                stage[to, :size, cols] = total.astype(BF16)

            @pl.when(jnp.logical_not(own))
            def _():
                other_copy(c, t, arrived).start()

            for at in RING:
                @pl.when(t == at)
                def _(at=at):
                    ring_copy(c, at).start()

            return 0

        def dn_own(t, _):
            for k, part in enumerate(dn_dots(t)):
                kept[t - STAGED, :size, k * GU:(k + 1) * GU] = part
            return 0

        lax.fori_loop(0, STAGED, dn_step, 0)
        lax.fori_loop(STAGED, TILES, dn_own, 0)

    for c in range(chunks):
        one_chunk(c)
    finish(last)
    forward1(last)
    forward2(last)
    sent(last)
    half = 1 - core
    for c in range(chunks):
        for k, dst in ((4, out(c, chip, half)), (7, out(c, prv, half)), (8, out(c, nxt, half)),
                       (9, out(c, far, half, 0)), (10, out(c, far, half, 1))):
            gather_wait(c, k, dst)


def solution(mesh):
    chips = mesh.shape["tp"] // 2

    def step(x, w_gate, w_up, w_down):
        n, d = x.shape
        ff = w_gate.shape[1]
        sizes = tuple(share * n // sum(SHARES) for share in SHARES)
        chunks, size = len(sizes), max(sizes)
        dma = pltpu.SemaphoreType.DMA
        hbm = pl.BlockSpec(memory_space=pl.ANY)
        return pl.pallas_call(
            functools.partial(kernel, chips, sizes),
            out_shape=jax.ShapeDtypeStruct((n, d), BF16),
            in_specs=[hbm] * 4,
            out_specs=hbm,
            scratch_shapes=[
                pltpu.VMEM((size, d), BF16),
                pltpu.VMEM((size, ff), BF16),
                pltpu.VMEM((SLOTS, d, GU), BF16),
                pltpu.VMEM((2, size, DN), F32),
                pltpu.VMEM((TILES // 2 + 1, size, DN), BF16),
                pltpu.VMEM((FIRST + 1, size, DN), BF16),
                pltpu.VMEM((4, size, DN), BF16),
                pltpu.VMEM((STAGES, size, DN), BF16),
                pltpu.VMEM((size, 2 * DN), BF16),
                dma, dma((SLOTS,)),
                dma((STAGES,)),
                dma((chunks, TILES // 2)),
                dma((chunks, FIRST + 4)),
                dma((12,)),
                dma((chunks, 11)),
                pltpu.SemaphoreType.REGULAR((3,)),
            ],
            compiler_params=pltpu.CompilerParams(
                collective_id=0, has_side_effects=True, vmem_limit_bytes=67043328),
            cost_estimate=pl.CostEstimate(flops=6 * n * d * ff, bytes_accessed=chunks * 6 * d * ff, transcendentals=n * ff),
        )(x, w_gate, w_up, w_down)

    return jax.shard_map(
        step,
        mesh=mesh,
        in_specs=(P("dp", None), P(None, "tp"), P(None, "tp"), P("tp", None)),
        out_specs=P("dp", None),
        check_vma=False,
    )
```

time: 835 us -> 529 us (0.63)
  Pallas kernels: 0 us -> 506 us
  matrix products: 463 us -> 0 us
  waiting for transfers between devices: 335 us -> 0 us
  between operations: 13.4 us -> 0.01 us
    pallas_call x0 -> x1, Pallas kernels: none -> 506 us  [step(): pl.pallas_call(functools.partial(kernel, chips, sizes), out_shape=jax.Sha...]
    dot_general x3 -> x0, matrix products: 463 us -> none  [the longest x1 160 us: step(): up = jnp.dot(x, w_up, preferred_element_type=jnp.float32)]
    psum x1 -> x0, waiting for transfers between devices: 335 us -> none  [step(): return lax.psum(term, 'tp')]
  transfers between devices with their start and end apart: 1 -> 0, of which waited for: 1 -> 0; matrix products, arithmetic and copies ran while one was open for 0% -> 0% of each run, Pallas kernels for 0% -> 0%
where the time goes in v2:
time: 529 us
  Pallas kernels  506 us (96%)
  local copies, waits for them, and re-layouts  23 us (4%)
    pallas_call x1, Pallas kernels, step(): pl.pallas_call(functools.partial(kernel, chips, sizes), out_shape=jax.Sha...  506 us
    unnamed x1, local copies, waits for them, and re-layouts  23 us

profile of v2, /device:TPU:113, one launch (start us, length us, event | category | flops | bytes accessed | tf_op | source)
XLA Modules:
  0.0 529.2 jit_solution(11145897964197421815)
XLA Ops:
  0.0 506.2 %shard_map.46 = bf16[2048,8192]{1,0:T(8,128)(2,1)} custom-call(bf16[2048,8192]{1,0:T(8,128)(2,1)} %x_ref.1, bf16[8192,4096]{1,0:T(8,128)(2,1)} %wg_ref.1, bf16[8192,4096]{1,0:T(8,128)(2,1)} %wu_ref.1, bf16[4096,8192]{1,0:T(8,128)(2,1)} %wd_ref.1), custom_call_target="tpu_custom_call" | custom-call | flops 412316860416 | bytes 805306368 | tf_op jit(solution)/shard_map/pallas_call | solution.py:331
  506.2 23.0 %copy.6 = bf16[2048,8192]{1,0:T(8,128)(2,1)} copy(bf16[2048,8192]{1,0:T(8,128)(2,1)} %shard_map.46) | data formatting | bytes 67108864
